TPU v7x, 256 devices: a whole 4x4x8 slice. The times are simulated.
256 devices in a mesh: rows: 128 (over z, y, x), sub: 2 (over core).
Axes of the slice: x: 4, y: 4, z: 8, core: 2. Of those that a mesh axis runs over, the one named last changes fastest.
Arguments:
- matrix: float32 [32768, 384], P(('rows', 'sub')), as said below
- grad_out: float32 [32768, 384], P(('rows', 'sub')), as said below
- grad_factor: float32 [384, 384], replicated, may hold values from -6 to 6
Outputs:
- grad_matrix: float32 [32768, 384], P(('rows', 'sub'))
Inputs may be any that keep to these rules, and one draw needn't show every extreme that they name: `matrix`: entries at most of order 1 / sqrt(32768), with a scale that varies by row and by column. `grad_out`: entries of order 0.01.
All inputs are finite; a program needn't handle non-finite values.
Results may differ from a plain program's by a relative error of at most 0.0004.
Values sent between devices are 32-bit elements; how exact they have to be, the bound alone decides.
A program may use at most 64 MiB of HBM per device.

v0:
```python
import jax
import jax.numpy as jnp
from jax import lax
from jax.sharding import Mesh
from jax.sharding import PartitionSpec as P

SECTIONS = 2
ROWS_SUB = ("rows_0", "rows_1", "rows_2", "sub")


shift_frac = 0.02


def in_blocks(shard, dim, count):
    before, after = (shard.shape[:dim], shard.shape[dim + 1 :])
    return jnp.moveaxis(shard.reshape(*before, count, -1, *after), dim, 0)


def sum_at_owner(shard, axis, dim):
    tiles = in_blocks(shard, dim, lax.axis_size(axis))
    arrived = lax.all_to_all(tiles, axis, split_axis=0, concat_axis=0, tiled=True)
    return arrived.sum(axis=0)


def filled_up(lines, count):
    spare = -lines.shape[0] % count
    if not spare:
        return lines
    return jnp.concatenate([lines, jnp.zeros((spare, *lines.shape[1:]), lines.dtype)])


def sent_to_all(shard, axis):
    count = lax.axis_size(axis)
    return lax.all_to_all(
        jnp.broadcast_to(shard[None], (count, *shard.shape)), axis, 0, 0, tiled=True
    )


def laid_out(tiles, dim):
    dims = list(tiles.shape[1:])
    dims[dim] *= tiles.shape[0]
    return jnp.moveaxis(tiles, 0, dim).reshape(dims)


def gathered_by_axis(shard, axes, dim):
    far, near = axes
    leading = sent_to_all(shard, far)
    tiles = jnp.swapaxes(sent_to_all(leading, near), 0, 1)
    return laid_out(tiles.reshape(-1, *shard.shape), dim)


def sum_in_two_steps(shard, axes, dim):
    far, near = axes
    tiles = in_blocks(shard, dim, lax.axis_size(far))
    nearer = sum_at_owner(tiles, near, dim + 1)
    arrived = lax.all_to_all(nearer, far, split_axis=0, concat_axis=0, tiled=True)
    return arrived.sum(axis=0)


def total_of(shard, axes):
    lines = shard.reshape(-1)
    padded = filled_up(lines, lax.axis_size(axes[0]) * lax.axis_size(axes[1]))
    whole = gathered_by_axis(sum_in_two_steps(padded, axes, 0), axes, 0)
    return lax.slice_in_dim(whole, 0, len(lines)).reshape(shard.shape)


def gathered_copies(shard, axis, dim):
    return laid_out(sent_to_all(shard, axis), dim)


def full_dot(left, right):
    return jnp.dot(left, right, precision=lax.Precision.HIGHEST, preferred_element_type=jnp.float32)


def inner_gram(left, right):
    return lax.dot_general(
        left,
        right,
        (((0,), (0,)), ((), ())),
        precision=lax.Precision.HIGHEST,
        preferred_element_type=jnp.float32,
    )


def cholesky_adjoint(lower_fac, lower_inv, lower_grad):
    product = full_dot(lower_fac.T, lower_grad)
    phi_part = jnp.tril(product) - 0.5 * jnp.diag(jnp.diag(product))
    sandwich = full_dot(full_dot(lower_inv.T, phi_part), lower_inv)
    return 0.5 * (sandwich + sandwich.T)


def factor_grads(uppers, grad_factor):
    count = len(uppers)
    result = []
    for section_index in range(count):
        middle = grad_factor
        for later in range(section_index + 1, count):
            middle = full_dot(uppers[later].T, middle)
        for earlier in range(section_index - 1, -1, -1):
            middle = full_dot(middle, uppers[earlier].T)
        result.append(middle)
    return result


def summed_gram(partial_value):
    half_rows = sum_at_owner(partial_value, "sub", 0)
    half_rows = total_of(half_rows, (("rows_0", "rows_1"), "rows_2"))
    return gathered_copies(half_rows, "sub", 0)


def per_device(matrix, grad_out, grad_factor):
    width = matrix.shape[1]
    rate = shift_frac / width
    identity = jnp.eye(width, dtype=jnp.float32)
    current = matrix
    saved = []
    for section_index in range(SECTIONS):
        summed = summed_gram(inner_gram(current, current))
        shift_val = rate * jnp.trace(summed)
        lower_fac = jnp.linalg.cholesky(summed + shift_val * identity)
        lower_inv = lax.linalg.triangular_solve(lower_fac, identity, left_side=True, lower=True)
        following = full_dot(current, lower_inv.T)
        saved.append((current, following, lower_fac, lower_inv))
        current = following
    uppers = [item[2].T for item in saved]
    fac_grads = factor_grads(uppers, grad_factor)
    q_grad = grad_out
    for section_index in range(SECTIONS - 1, -1, -1):
        before, after, lower_fac, lower_inv = saved[section_index]
        crossed = total_of(inner_gram(after, q_grad), (("rows_0", "rows_1"), ("rows_2", "sub")))
        total_grad = fac_grads[section_index] - full_dot(crossed, lower_inv)
        gram_grad = cholesky_adjoint(lower_fac, lower_inv, jnp.tril(total_grad.T))
        gram_grad = gram_grad + rate * jnp.trace(gram_grad) * identity
        q_grad = full_dot(q_grad, lower_inv) + 2.0 * full_dot(before, gram_grad)
    return q_grad


def solution(mesh):
    torus = Mesh(
        mesh.devices.reshape(8, 4, 4, mesh.shape["sub"]), ("rows_0", "rows_1", "rows_2", "sub")
    )
    in_specs = (P(ROWS_SUB, None), P(ROWS_SUB, None), P())
    out_specs = P(ROWS_SUB, None)
    return jax.shard_map(
        per_device, mesh=torus, in_specs=in_specs, out_specs=out_specs, check_vma=False
    )
```

profile of v0, /device:TPU:1, one launch (start us, length us, event | category | flops | bytes accessed | tf_op | source)
XLA Modules:
  0.0 521.3 jit_solution(4658228563366612363)
XLA Ops:
  0.0 2.6 fusion.120
  2.6 6.7 %all-to-all-start = ((f32[2,192,384]{2,1,0:T(8,128)}), f32[2,192,384]{2,1,0:T(8,128)S(1)}, u32[]{:S(2)}, u32[]{:S(2)}) async-start(f32[2,192,384]{2,1,0:T(8,128)} %bitcast), calls=%async_computation | async-start | bytes 1179648 | tf_op jit(solution)/shard_map/all_to_all | solution.py:21
  11.0 9.2 %all_to_all.126 = f32[4,32,576]{2,1,0:T(8,128)S(1)} all-to-all(f32[4,32,576]{2,1,0:T(8,128)S(1)} %copy.45), channel_id=1, replica_groups=mesh['rows_0'=8,'rows_1'=4,'rows_2'=4,'sub'=2] {'rows_2'}, dimensions={0} | all-to-all | bytes 589824 | tf_op jit(solution)/shard_map/all_to_all | solution.py:21
  20.3 19.8 %all_to_all.127 = f32[32,1,576]{2,1,0:T(1,128)S(1)} all-to-all(f32[32,1,576]{2,1,0:T(1,128)S(1)} %all_to_all.78), channel_id=1, replica_groups=mesh['rows_0'=8,'rows_1'=4,'rows_2'=4,'sub'=2] {'rows_0','rows_1'}, dimensions={0} | all-to-all | bytes 147456 | tf_op jit(solution)/shard_map/all_to_all | solution.py:56
  40.8 3.9 all-to-all-start.3
  44.7 9.0 %all-to-all-done.3 = f32[32,1,576]{2,1,0:T(1,128)S(1)} async-done(((f32[32,1,576]{2,1,0:T(1,128)}), f32[32,1,576]{2,1,0:T(1,128)S(1)}, u32[]{:S(2)}, u32[]{:S(2)}) %all-to-all-start.3) | async-done | bytes 73760 | tf_op jit(solution)/shard_map/all_to_all | solution.py:34
  54.4 3.5 all-to-all-start.4
  57.9 5.8 %all-to-all-done.4 = f32[4,32,576]{2,1,0:T(8,128)S(1)} async-done(((f32[4,32,576]{2,1,0:T(8,128)}), f32[4,32,576]{2,1,0:T(8,128)S(1)}, u32[]{:S(2)}, u32[]{:S(2)}) %all-to-all-start.4) | async-done | bytes 294944 | tf_op jit(solution)/shard_map/all_to_all | solution.py:34
  64.3 9.1 %all_to_all.120 = f32[2,192,384]{2,1,0:T(8,128)S(1)} all-to-all(f32[2,192,384]{2,1,0:T(8,128)S(1)} %broadcast_in_dim.118), channel_id=1, replica_groups=mesh['rows_0'=8,'rows_1'=4,'rows_2'=4,'sub'=2] {'sub'}, dimensions={0} | all-to-all | bytes 1179648 | tf_op jit(solution)/shard_map/all_to_all | solution.py:34
  75.5 11.7 %cholesky.208 = f32[128,128]{1,0:T(8,128)S(1)} custom-call(f32[128,128]{1,0:T(8,128)S(1)} %cholesky.310), custom_call_target="Cholesky" | custom-call | tf_op jit(solution)/shard_map/jit(cholesky)/cholesky | solution.py:120
  87.2 9.8 %custom-call.24 = f32[1,128,128]{1,2,0:T(8,128)S(1)} custom-call(f32[1,128,128]{2,1,0:T(8,128)S(1)} %get-tuple-element.56), custom_call_target="InvertDiagBlocksLowerTriangular" | custom-call | tf_op jit(solution)/shard_map/jit(cholesky)/cholesky | solution.py:120
  97.6 11.7 %cholesky.227 = f32[128,128]{1,0:T(8,128)S(1)} custom-call(f32[128,128]{1,0:T(8,128)S(1)} %cholesky.314), custom_call_target="Cholesky" | custom-call | tf_op jit(solution)/shard_map/jit(cholesky)/cholesky | solution.py:120
  109.4 10.0 %custom-call.25 = f32[1,128,128]{1,2,0:T(8,128)S(1)} custom-call(f32[1,128,128]{2,1,0:T(8,128)S(1)} %get-tuple-element.53), custom_call_target="InvertDiagBlocksLowerTriangular" | custom-call | tf_op jit(solution)/shard_map/jit(cholesky)/cholesky | solution.py:120
  119.9 11.7 %cholesky.246 = f32[128,128]{1,0:T(8,128)S(1)} custom-call(f32[128,128]{1,0:T(8,128)S(1)} %convolution_subtract_fusion.9), custom_call_target="Cholesky" | custom-call | tf_op jit(solution)/shard_map/jit(cholesky)/cholesky | solution.py:120
  134.9 6.4 %while.4 = (s32[]{:T(128)}, f32[384,384]{1,0:T(8,128)S(1)}, s32[3,2]{0,1:T(2,128)S(1)}, f32[3,128,128]{2,1,0:T(8,128)S(1)}, s32[]{:T(128)}) while((s32[]{:T(128)}, f32[384,384]{1,0:T(8,128)S(1)}, s32[3,2]{0,1:T(2,128)S(1)}, f32[3,128,128]{2,1,0:T(8,128)S(1)}, s32[]{:T(128)}) %tuple.47), condition=%wide.while_cond, body=%wide.while_body.sunk | while | flops 2 | bytes 131181 | solution.py:121
  135.6 1.4 bitcast_dynamic-update-slice_fusion.4
  137.7 1.4 bitcast_dynamic-update-slice_fusion.4
  141.3 29.5 %custom-call.26 = f32[3,128,128]{1,2,0:T(8,128)S(1)} custom-call(f32[3,128,128]{2,1,0:T(8,128)S(1)} %get-tuple-element.21), custom_call_target="InvertDiagBlocksLowerTriangular" | custom-call | tf_op jit(solution)/shard_map/triangular_solve/custom-call.2 | solution.py:121
  175.1 4.2 all_to_all.121
  181.4 9.2 %all_to_all.128 = f32[4,32,576]{2,1,0:T(8,128)S(1)} all-to-all(f32[4,32,576]{2,1,0:T(8,128)S(1)} %copy.51), channel_id=1, replica_groups=mesh['rows_0'=8,'rows_1'=4,'rows_2'=4,'sub'=2] {'rows_2'}, dimensions={0} | all-to-all | bytes 589824 | tf_op jit(solution)/shard_map/all_to_all | solution.py:21
  190.6 12.0 %all_to_all.129 = f32[32,1,576]{2,1,0:T(1,128)S(1)} all-to-all(f32[32,1,576]{2,1,0:T(1,128)S(1)} %all_to_all.85), channel_id=1, replica_groups=mesh['rows_0'=8,'rows_1'=4,'rows_2'=4,'sub'=2] {'rows_0','rows_1'}, dimensions={0} | all-to-all | bytes 147456 | tf_op jit(solution)/shard_map/all_to_all | solution.py:56
  202.7 12.0 %all_to_all.122 = f32[32,1,576]{2,1,0:T(1,128)S(1)} all-to-all(f32[32,1,576]{2,1,0:T(1,128)S(1)} %broadcast_in_dim.120), channel_id=1, replica_groups=mesh['rows_0'=8,'rows_1'=4,'rows_2'=4,'sub'=2] {'rows_0','rows_1'}, dimensions={0} | all-to-all | bytes 147456 | tf_op jit(solution)/shard_map/all_to_all | solution.py:34
  214.8 8.3 %all_to_all.130 = f32[4,32,576]{2,1,0:T(8,128)S(1)} all-to-all(f32[4,32,576]{2,1,0:T(8,128)S(1)} %broadcast_in_dim.122), channel_id=1, replica_groups=mesh['rows_0'=8,'rows_1'=4,'rows_2'=4,'sub'=2] {'rows_2'}, dimensions={0} | all-to-all | bytes 589824 | tf_op jit(solution)/shard_map/all_to_all | solution.py:34
  225.2 9.0 %all_to_all.123 = f32[2,192,384]{2,1,0:T(8,128)S(1)} all-to-all(f32[2,192,384]{2,1,0:T(8,128)S(1)} %broadcast_in_dim.124), channel_id=1, replica_groups=mesh['rows_0'=8,'rows_1'=4,'rows_2'=4,'sub'=2] {'sub'}, dimensions={0} | all-to-all | bytes 1179648 | tf_op jit(solution)/shard_map/all_to_all | solution.py:34
  236.7 2.0 select_add_fusion
  238.7 2.2 copy.54
  242.8 11.7 %cholesky.261 = f32[128,128]{1,0:T(8,128)S(1)} custom-call(f32[128,128]{1,0:T(8,128)S(1)} %cholesky.318), custom_call_target="Cholesky" | custom-call | tf_op jit(solution)/shard_map/jit(cholesky)/cholesky | solution.py:120
  254.6 9.8 %custom-call.27 = f32[1,128,128]{1,2,0:T(8,128)S(1)} custom-call(f32[1,128,128]{2,1,0:T(8,128)S(1)} %get-tuple-element.49), custom_call_target="InvertDiagBlocksLowerTriangular" | custom-call | tf_op jit(solution)/shard_map/jit(cholesky)/cholesky | solution.py:120
  266.8 11.7 %cholesky.280 = f32[128,128]{1,0:T(8,128)S(1)} custom-call(f32[128,128]{1,0:T(8,128)S(1)} %cholesky.322), custom_call_target="Cholesky" | custom-call | tf_op jit(solution)/shard_map/jit(cholesky)/cholesky | solution.py:120
  279.8 10.0 %custom-call.28 = f32[1,128,128]{1,2,0:T(8,128)S(1)} custom-call(f32[1,128,128]{2,1,0:T(8,128)S(1)} %get-tuple-element.46), custom_call_target="InvertDiagBlocksLowerTriangular" | custom-call | tf_op jit(solution)/shard_map/jit(cholesky)/cholesky | solution.py:120
  291.1 11.7 %cholesky.299 = f32[128,128]{1,0:T(8,128)S(1)} custom-call(f32[128,128]{1,0:T(8,128)S(1)} %convolution_subtract_fusion.8), custom_call_target="Cholesky" | custom-call | tf_op jit(solution)/shard_map/jit(cholesky)/cholesky | solution.py:120
  306.3 8.4 %while.5 = (s32[]{:T(128)}, f32[384,384]{1,0:T(8,128)}, s32[3,2]{0,1:T(2,128)S(1)}, f32[3,128,128]{2,1,0:T(8,128)S(1)}, s32[]{:T(128)}) while((s32[]{:T(128)}, f32[384,384]{1,0:T(8,128)}, s32[3,2]{0,1:T(2,128)S(1)}, f32[3,128,128]{2,1,0:T(8,128)S(1)}, s32[]{:T(128)}) %tuple.53), condition=%wide.while_cond.clone, body=%wide.while_body.clone.sunk | while | flops 2 | bytes 131181 | solution.py:121
  306.9 2.2 bitcast_dynamic-update-slice_fusion.5
  309.8 2.2 bitcast_dynamic-update-slice_fusion.5
  312.6 2.1 bitcast_dynamic-update-slice_fusion.5
  314.7 29.5 %custom-call.29 = f32[3,128,128]{1,2,0:T(8,128)S(1)} custom-call(f32[3,128,128]{2,1,0:T(8,128)S(1)} %get-tuple-element.22), custom_call_target="InvertDiagBlocksLowerTriangular" | custom-call | tf_op jit(solution)/shard_map/triangular_solve/custom-call.2 | solution.py:121
  347.5 1.7 convolution_subtract_fusion.2
  351.5 1.5 fusion.122
  353.0 2.2 reshape_reshape_reshape.20
  356.4 14.6 %all_to_all.131 = f32[8,32,576]{2,1,0:T(8,128)} all-to-all(f32[8,32,576]{2,1,0:T(8,128)S(1)} %bitcast.156), channel_id=1, replica_groups=mesh['rows_0'=8,'rows_1'=4,'rows_2'=4,'sub'=2] {'rows_2','sub'}, dimensions={0} | all-to-all | bytes 1179648 | tf_op jit(solution)/shard_map/all_to_all | solution.py:21
  372.2 12.1 %all_to_all.132 = f32[32,1,576]{2,1,0:T(1,128)S(1)} all-to-all(f32[32,1,576]{2,1,0:T(1,128)S(1)} %all_to_all.91), channel_id=1, replica_groups=mesh['rows_0'=8,'rows_1'=4,'rows_2'=4,'sub'=2] {'rows_0','rows_1'}, dimensions={0} | all-to-all | bytes 147456 | tf_op jit(solution)/shard_map/all_to_all | solution.py:56
  384.3 11.9 %all_to_all.124 = f32[32,1,576]{2,1,0:T(1,128)S(1)} all-to-all(f32[32,1,576]{2,1,0:T(1,128)S(1)} %broadcast_in_dim.125), channel_id=1, replica_groups=mesh['rows_0'=8,'rows_1'=4,'rows_2'=4,'sub'=2] {'rows_0','rows_1'}, dimensions={0} | all-to-all | bytes 147456 | tf_op jit(solution)/shard_map/all_to_all | solution.py:34
  397.2 7.4 %all-to-all-start.15 = ((f32[8,32,576]{2,1,0:T(8,128)}), f32[8,32,576]{2,1,0:T(8,128)}, u32[]{:S(2)}, u32[]{:S(2)}) async-start(f32[8,32,576]{2,1,0:T(8,128)} %broadcast_in_dim.127), calls=%async_computation.15 | async-start | bytes 1310720 | tf_op jit(solution)/shard_map/all_to_all | solution.py:34
  404.6 2.1 fusion.38
  406.7 8.7 %all-to-all-done.15 = f32[8,32,576]{2,1,0:T(8,128)} async-done(((f32[8,32,576]{2,1,0:T(8,128)}), f32[8,32,576]{2,1,0:T(8,128)}, u32[]{:S(2)}, u32[]{:S(2)}) %all-to-all-start.15) | async-done | bytes 589856 | tf_op jit(solution)/shard_map/all_to_all | solution.py:34
  415.5 2.3 copy.58
  417.8 2.3 reshape_reshape_reshape.21
  420.1 2.5 fusion
  422.6 1.5 fusion.34
  425.2 3.8 gather_fusion
  429.0 3.3 fusion.21
  434.7 1.7 select_reduce_fusion.1
  437.0 1.8 convolution_multiply_fusion.1
  443.6 15.0 %all_to_all.133 = f32[8,32,576]{2,1,0:T(8,128)} all-to-all(f32[8,32,576]{2,1,0:T(8,128)S(1)} %bitcast.157), channel_id=1, replica_groups=mesh['rows_0'=8,'rows_1'=4,'rows_2'=4,'sub'=2] {'rows_2','sub'}, dimensions={0} | all-to-all | bytes 1179648 | tf_op jit(solution)/shard_map/all_to_all | solution.py:21
  459.8 12.0 %all_to_all.134 = f32[32,1,576]{2,1,0:T(1,128)S(1)} all-to-all(f32[32,1,576]{2,1,0:T(1,128)S(1)} %all_to_all.96), channel_id=1, replica_groups=mesh['rows_0'=8,'rows_1'=4,'rows_2'=4,'sub'=2] {'rows_0','rows_1'}, dimensions={0} | all-to-all | bytes 147456 | tf_op jit(solution)/shard_map/all_to_all | solution.py:56
  471.9 12.1 %all_to_all.125 = f32[32,1,576]{2,1,0:T(1,128)S(1)} all-to-all(f32[32,1,576]{2,1,0:T(1,128)S(1)} %broadcast_in_dim.129), channel_id=1, replica_groups=mesh['rows_0'=8,'rows_1'=4,'rows_2'=4,'sub'=2] {'rows_0','rows_1'}, dimensions={0} | all-to-all | bytes 147456 | tf_op jit(solution)/shard_map/all_to_all | solution.py:34
  484.8 7.6 %all-to-all-start.19 = ((f32[8,32,576]{2,1,0:T(8,128)}), f32[8,32,576]{2,1,0:T(8,128)}, u32[]{:S(2)}, u32[]{:S(2)}) async-start(f32[8,32,576]{2,1,0:T(8,128)} %broadcast_in_dim.131), calls=%async_computation.19 | async-start | bytes 1310720 | tf_op jit(solution)/shard_map/all_to_all | solution.py:34
  492.5 2.1 convolution_bitcast_fusion
  494.6 8.7 %all-to-all-done.19 = f32[8,32,576]{2,1,0:T(8,128)} async-done(((f32[8,32,576]{2,1,0:T(8,128)}), f32[8,32,576]{2,1,0:T(8,128)}, u32[]{:S(2)}, u32[]{:S(2)}) %all-to-all-start.19) | async-done | bytes 589856 | tf_op jit(solution)/shard_map/all_to_all | solution.py:34
  503.3 1.5 copy.65
  506.0 2.6 fusion.1
  508.6 1.5 fusion.36
  510.3 3.4 gather_fusion.1
  513.8 2.1 fusion.14
  (145 shorter events, 57.6 us)
Async XLA Ops:
  0.0 404.6 %copy-start = (f32[384,384]{1,0:T(8,128)S(1)}, f32[384,384]{1,0:T(8,128)}, u32[]{:S(2)}) copy-start(f32[384,384]{1,0:T(8,128)} %param.8) | copy-start | bytes 1769476
  2.6 8.1 %all-to-all-start = ((f32[2,192,384]{2,1,0:T(8,128)}), f32[2,192,384]{2,1,0:T(8,128)S(1)}, u32[]{:S(2)}, u32[]{:S(2)}) async-start(f32[2,192,384]{2,1,0:T(8,128)} %bitcast), calls=%async_computation | async-start | bytes 1179648 | tf_op jit(solution)/shard_map/all_to_all | solution.py:21
  40.8 12.9 %all-to-all-start.3 = ((f32[32,1,576]{2,1,0:T(1,128)}), f32[32,1,576]{2,1,0:T(1,128)S(1)}, u32[]{:S(2)}, u32[]{:S(2)}) async-start(f32[32,1,576]{2,1,0:T(1,128)} %broadcast_in_dim.114), calls=%async_computation.3 | async-start | bytes 163840 | tf_op jit(solution)/shard_map/all_to_all | solution.py:34
  54.4 9.3 %all-to-all-start.4 = ((f32[4,32,576]{2,1,0:T(8,128)}), f32[4,32,576]{2,1,0:T(8,128)S(1)}, u32[]{:S(2)}, u32[]{:S(2)}) async-start(f32[4,32,576]{2,1,0:T(8,128)} %broadcast_in_dim.116), calls=%async_computation.4 | async-start | bytes 655360 | tf_op jit(solution)/shard_map/all_to_all | solution.py:34
  172.9 0.9 copy-start.5
  238.7 2.2 copy-start.1
  242.0 0.8 copy-start.9
  344.2 0.7 copy-start.12
  350.4 69.7 %copy-start.2 = (f32[128,384]{1,0:T(8,128)}, f32[128,384]{1,0:T(8,128)S(1)}, u32[]{:S(2)}) copy-start(f32[128,384]{1,0:T(8,128)S(1)} %fusion.76) | copy-start | bytes 589828
  350.5 1.0 copy-start.10
  397.2 18.3 %all-to-all-start.15 = ((f32[8,32,576]{2,1,0:T(8,128)}), f32[8,32,576]{2,1,0:T(8,128)}, u32[]{:S(2)}, u32[]{:S(2)}) async-start(f32[8,32,576]{2,1,0:T(8,128)} %broadcast_in_dim.127), calls=%async_computation.15 | async-start | bytes 1310720 | tf_op jit(solution)/shard_map/all_to_all | solution.py:34
  429.0 3.3 copy-start.3
  436.9 1.8 copy-start.4
  437.0 1.8 copy-start.11
  439.9 0.7 copy-start.7
  484.8 18.5 %all-to-all-start.19 = ((f32[8,32,576]{2,1,0:T(8,128)}), f32[8,32,576]{2,1,0:T(8,128)}, u32[]{:S(2)}, u32[]{:S(2)}) async-start(f32[8,32,576]{2,1,0:T(8,128)} %broadcast_in_dim.131), calls=%async_computation.19 | async-start | bytes 1310720 | tf_op jit(solution)/shard_map/all_to_all | solution.py:34
  517.4 1.4 copy-start.6
  518.8 0.9 copy-start.8
where the time goes:
time: 526 us; the launch traced here: 521 us
  other arithmetic  184 us (35%)
  blocking collectives  170 us (32%)
  local copies, waits for them, and re-layouts  51.9 us (10%)
  matrix products  45.1 us (9%)
  waiting for transfers between devices  33.7 us (6%)
  starting transfers between devices  29 us (6%)
  between operations  7.28 us (1%)
    another operation x21, other arithmetic, per_device(): lower_fac = jnp.linalg.cholesky(summed + shift_val * identity)  113 us
    all_to_all x6, blocking collectives, sent_to_all(): lax.all_to_all(jnp.broadcast_to(shard[None], (count, *shard.shape)), axis...  62.3 us
    another operation x5, other arithmetic, per_device(): lax.linalg.triangular_solve(lower_fac, identity, left_side=True, lower=True)  59.9 us
    all_to_all x4, blocking collectives, sum_in_two_steps(): lax.all_to_all(nearer, far, split_axis=0, concat_axis=0, tiled=True)  55.8 us
    all_to_all x5, blocking collectives, sum_at_owner(): lax.all_to_all(tiles, axis, split_axis=0, concat_axis=0, tiled=True)  52.1 us
    all_to_all x4, waiting for transfers between devices, sent_to_all(): lax.all_to_all(jnp.broadcast_to(shard[None], (count, *shard.shape)), axis...  32.2 us
    dot_general x16, matrix products, full_dot(): jnp.dot(left, right, precision=lax.Precision.HIGHEST, preferred_element_t...  26.7 us
    all_to_all x4, starting transfers between devices, sent_to_all(): lax.all_to_all(jnp.broadcast_to(shard[None], (count, *shard.shape)), axis...  22.3 us
  transfers between devices with their start and end apart: 5, of which 5 were waited for; matrix products, arithmetic and copies ran while one was open for 1% of the time, Pallas kernels for 0%

commit v1 on v0

--- a/solution.py
+++ b/solution.py
@@ -112,27 +112,32 @@
     width = matrix.shape[1]
     rate = shift_frac / width
     identity = jnp.eye(width, dtype=jnp.float32)
-    current = matrix
-    saved = []
-    for section_index in range(SECTIONS):
-        summed = summed_gram(inner_gram(current, current))
+
+    def factored(summed):
         shift_val = rate * jnp.trace(summed)
         lower_fac = jnp.linalg.cholesky(summed + shift_val * identity)
         lower_inv = lax.linalg.triangular_solve(lower_fac, identity, left_side=True, lower=True)
-        following = full_dot(current, lower_inv.T)
-        saved.append((current, following, lower_fac, lower_inv))
-        current = following
-    uppers = [item[2].T for item in saved]
+        return lower_fac, lower_inv
+
+    def gram_cotangent(total_grad, lower_fac, lower_inv):
+        gram_grad = cholesky_adjoint(lower_fac, lower_inv, jnp.tril(total_grad.T))
+        return gram_grad + rate * jnp.trace(gram_grad) * identity
+
+    first_fac, first_inv = factored(summed_gram(inner_gram(matrix, matrix)))
+    middle = full_dot(matrix, first_inv.T)
+    both = summed_gram(inner_gram(middle, jnp.concatenate([middle, grad_out], axis=1)))
+    second_gram, crossed = both[:, :width], both[:, width:]
+    second_fac, second_inv = factored(second_gram)
+
+    uppers = [first_fac.T, second_fac.T]
     fac_grads = factor_grads(uppers, grad_factor)
-    q_grad = grad_out
-    for section_index in range(SECTIONS - 1, -1, -1):
-        before, after, lower_fac, lower_inv = saved[section_index]
-        crossed = total_of(inner_gram(after, q_grad), (("rows_0", "rows_1"), ("rows_2", "sub")))
-        total_grad = fac_grads[section_index] - full_dot(crossed, lower_inv)
-        gram_grad = cholesky_adjoint(lower_fac, lower_inv, jnp.tril(total_grad.T))
-        gram_grad = gram_grad + rate * jnp.trace(gram_grad) * identity
-        q_grad = full_dot(q_grad, lower_inv) + 2.0 * full_dot(before, gram_grad)
-    return q_grad
+    second_total = fac_grads[1] - full_dot(full_dot(second_inv, crossed), second_inv)
+    second_weight = gram_cotangent(second_total, second_fac, second_inv)
+    first_cross = full_dot(crossed, second_inv) + 2.0 * full_dot(second_gram, second_weight)
+    first_total = fac_grads[0] - full_dot(first_cross, first_inv)
+    first_weight = gram_cotangent(first_total, first_fac, first_inv)
+    middle_grad = full_dot(grad_out, second_inv) + 2.0 * full_dot(middle, second_weight)
+    return full_dot(middle_grad, first_inv) + 2.0 * full_dot(matrix, first_weight)
 
 
 def solution(mesh):

time: 526 us -> 406 us (0.77)
  blocking collectives: 170 us -> 90.4 us
  local copies, waits for them, and re-layouts: 51.9 us -> 37.6 us
  waiting for transfers between devices: 33.7 us -> 20.5 us
  starting transfers between devices: 29 us -> 17.5 us
    all_to_all x6 -> x3, blocking collectives: 62.3 us -> 31.3 us  [sent_to_all(): lax.all_to_all(jnp.broadcast_to(shard[None], (count, *shard.shape)), axis...]
    all_to_all x5 -> x3, blocking collectives: 52.1 us -> 26.8 us  [sum_at_owner(): lax.all_to_all(tiles, axis, split_axis=0, concat_axis=0, tiled=True)]
    all_to_all x4 -> x2, blocking collectives: 55.8 us -> 32.3 us  [sum_in_two_steps(): lax.all_to_all(nearer, far, split_axis=0, concat_axis=0, tiled=True)]
    all_to_all x4 -> x3, waiting for transfers between devices: 32.2 us -> 19.1 us  [sent_to_all(): lax.all_to_all(jnp.broadcast_to(shard[None], (count, *shard.shape)), axis...]
    all_to_all x4 -> x3, starting transfers between devices: 22.3 us -> 10.8 us  [sent_to_all(): lax.all_to_all(jnp.broadcast_to(shard[None], (count, *shard.shape)), axis...]
    another operation x6 -> x2, local copies, waits for them, and re-layouts: 7.34 us -> 0.54 us  [in_blocks(): return jnp.moveaxis(shard.reshape(*before, count, -1, *after), dim, 0)]
    another operation x29 -> x27, local copies, waits for them, and re-layouts: 18.3 us -> 15.1 us  [the longest x21 15 us: factored(): lax.linalg.triangular_solve(lower_fac, identity, left_side=True, lower=True)]
    dot_general x16 -> x18, matrix products: 26.7 us -> 27.1 us  [full_dot(): jnp.dot(left, right, precision=lax.Precision.HIGHEST, preferred_element_t...]
  transfers between devices with their start and end apart: 5 -> 4, of which waited for: 5 -> 4; matrix products, arithmetic and copies ran while one was open for 1% -> 1% of each run, Pallas kernels for 0% -> 0%
where the time goes in v1:
time: 406 us; the launch traced here: 402 us
  other arithmetic  182 us (45%)
  blocking collectives  90.4 us (22%)
  matrix products  46.6 us (11%)
  local copies, waits for them, and re-layouts  37.6 us (9%)
  waiting for transfers between devices  20.5 us (5%)
  starting transfers between devices  17.5 us (4%)
  between operations  7.49 us (2%)
    another operation x21, other arithmetic, factored(): lower_fac = jnp.linalg.cholesky(summed + shift_val * identity)  114 us
    another operation x5, other arithmetic, factored(): lax.linalg.triangular_solve(lower_fac, identity, left_side=True, lower=True)  59.9 us
    all_to_all x2, blocking collectives, sum_in_two_steps(): lax.all_to_all(nearer, far, split_axis=0, concat_axis=0, tiled=True)  32.3 us
    all_to_all x3, blocking collectives, sent_to_all(): lax.all_to_all(jnp.broadcast_to(shard[None], (count, *shard.shape)), axis...  31.3 us
    dot_general x18, matrix products, full_dot(): jnp.dot(left, right, precision=lax.Precision.HIGHEST, preferred_element_t...  27.1 us
    all_to_all x3, blocking collectives, sum_at_owner(): lax.all_to_all(tiles, axis, split_axis=0, concat_axis=0, tiled=True)  26.8 us
    all_to_all x3, waiting for transfers between devices, sent_to_all(): lax.all_to_all(jnp.broadcast_to(shard[None], (count, *shard.shape)), axis...  19.1 us
    another operation x21, local copies, waits for them, and re-layouts, factored(): lax.linalg.triangular_solve(lower_fac, identity, left_side=True, lower=True)  15 us
  transfers between devices with their start and end apart: 4, of which 4 were waited for; matrix products, arithmetic and copies ran while one was open for 1% of the time, Pallas kernels for 0%

profile of v1, /device:TPU:1, one launch (start us, length us, event | category | flops | bytes accessed | tf_op | source)
XLA Modules:
  0.0 401.9 jit_solution(16811357438355903361)
XLA Ops:
  0.0 2.6 fusion.129
  2.6 6.7 %all-to-all-start = ((f32[2,192,384]{2,1,0:T(8,128)}), f32[2,192,384]{2,1,0:T(8,128)S(1)}, u32[]{:S(2)}, u32[]{:S(2)}) async-start(f32[2,192,384]{2,1,0:T(8,128)} %bitcast), calls=%async_computation | async-start | bytes 1179648 | tf_op jit(solution)/shard_map/all_to_all | solution.py:21
  9.3 1.4 all-to-all-done
  11.0 9.3 %all_to_all.74 = f32[4,32,576]{2,1,0:T(8,128)S(1)} all-to-all(f32[4,32,576]{2,1,0:T(8,128)S(1)} %copy.42), channel_id=1, replica_groups=mesh['rows_0'=8,'rows_1'=4,'rows_2'=4,'sub'=2] {'rows_2'}, dimensions={0} | all-to-all | bytes 589824 | tf_op jit(solution)/shard_map/all_to_all | solution.py:21
  20.4 19.8 %all_to_all.75 = f32[32,1,576]{2,1,0:T(1,128)S(1)} all-to-all(f32[32,1,576]{2,1,0:T(1,128)S(1)} %all_to_all.46), channel_id=1, replica_groups=mesh['rows_0'=8,'rows_1'=4,'rows_2'=4,'sub'=2] {'rows_0','rows_1'}, dimensions={0} | all-to-all | bytes 147456 | tf_op jit(solution)/shard_map/all_to_all | solution.py:56
  41.0 3.9 all-to-all-start.3
  45.7 8.2 %all-to-all-done.3 = f32[32,1,576]{2,1,0:T(1,128)S(1)} async-done(((f32[32,1,576]{2,1,0:T(1,128)}), f32[32,1,576]{2,1,0:T(1,128)S(1)}, u32[]{:S(2)}, u32[]{:S(2)}) %all-to-all-start.3) | async-done | bytes 73760 | tf_op jit(solution)/shard_map/all_to_all | solution.py:34
  54.6 3.5 all-to-all-start.4
  58.1 5.8 %all-to-all-done.4 = f32[4,32,576]{2,1,0:T(8,128)S(1)} async-done(((f32[4,32,576]{2,1,0:T(8,128)}), f32[4,32,576]{2,1,0:T(8,128)S(1)}, u32[]{:S(2)}, u32[]{:S(2)}) %all-to-all-start.4) | async-done | bytes 294944 | tf_op jit(solution)/shard_map/all_to_all | solution.py:34
  64.4 9.1 %all_to_all.70 = f32[2,192,384]{2,1,0:T(8,128)S(1)} all-to-all(f32[2,192,384]{2,1,0:T(8,128)S(1)} %broadcast_in_dim.90), channel_id=1, replica_groups=mesh['rows_0'=8,'rows_1'=4,'rows_2'=4,'sub'=2] {'sub'}, dimensions={0} | all-to-all | bytes 1179648 | tf_op jit(solution)/shard_map/all_to_all | solution.py:34
  76.5 11.7 %cholesky.208 = f32[128,128]{1,0:T(8,128)S(1)} custom-call(f32[128,128]{1,0:T(8,128)S(1)} %cholesky.310), custom_call_target="Cholesky" | custom-call | tf_op jit(solution)/shard_map/jit(cholesky)/cholesky | solution.py:118
  88.3 9.8 %custom-call.24 = f32[1,128,128]{1,2,0:T(8,128)S(1)} custom-call(f32[1,128,128]{2,1,0:T(8,128)S(1)} %get-tuple-element.56), custom_call_target="InvertDiagBlocksLowerTriangular" | custom-call | tf_op jit(solution)/shard_map/jit(cholesky)/cholesky | solution.py:118
  99.3 1.2 convolution_subtract_fusion.7
  100.5 11.7 %cholesky.227 = f32[128,128]{1,0:T(8,128)S(1)} custom-call(f32[128,128]{1,0:T(8,128)S(1)} %cholesky.314), custom_call_target="Cholesky" | custom-call | tf_op jit(solution)/shard_map/jit(cholesky)/cholesky | solution.py:118
  112.2 10.2 %custom-call.25 = f32[1,128,128]{1,2,0:T(8,128)S(1)} custom-call(f32[1,128,128]{2,1,0:T(8,128)S(1)} %get-tuple-element.53), custom_call_target="InvertDiagBlocksLowerTriangular" | custom-call | tf_op jit(solution)/shard_map/jit(cholesky)/cholesky | solution.py:118
  123.8 11.7 %cholesky.246 = f32[128,128]{1,0:T(8,128)S(1)} custom-call(f32[128,128]{1,0:T(8,128)S(1)} %convolution_subtract_fusion.9), custom_call_target="Cholesky" | custom-call | tf_op jit(solution)/shard_map/jit(cholesky)/cholesky | solution.py:118
  139.0 6.4 %while.4 = (s32[]{:T(128)}, f32[384,384]{1,0:T(8,128)S(1)}, s32[3,2]{0,1:T(2,128)S(1)}, f32[3,128,128]{2,1,0:T(8,128)S(1)}, s32[]{:T(128)}) while((s32[]{:T(128)}, f32[384,384]{1,0:T(8,128)S(1)}, s32[3,2]{0,1:T(2,128)S(1)}, f32[3,128,128]{2,1,0:T(8,128)S(1)}, s32[]{:T(128)}) %tuple.47), condition=%wide.while_cond, body=%wide.while_body.sunk | while | flops 2 | bytes 131181 | solution.py:119
  139.7 1.4 bitcast_dynamic-update-slice_fusion.4
  141.8 1.4 bitcast_dynamic-update-slice_fusion.4
  143.9 1.4 bitcast_dynamic-update-slice_fusion.4
  145.4 29.5 %custom-call.26 = f32[3,128,128]{1,2,0:T(8,128)S(1)} custom-call(f32[3,128,128]{2,1,0:T(8,128)S(1)} %get-tuple-element.21), custom_call_target="InvertDiagBlocksLowerTriangular" | custom-call | tf_op jit(solution)/shard_map/triangular_solve/custom-call.2 | solution.py:119
  179.2 5.5 %all_to_all.71 = f32[2,192,768]{2,1,0:T(8,128)} all-to-all(f32[2,192,768]{2,1,0:T(8,128)S(1)} %bitcast.143), channel_id=1, replica_groups=mesh['rows_0'=8,'rows_1'=4,'rows_2'=4,'sub'=2] {'sub'}, dimensions={0} | all-to-all | bytes 2359296 | tf_op jit(solution)/shard_map/all_to_all | solution.py:21
  184.7 1.4 reduce_sum.86
  186.5 12.0 %all_to_all.76 = f32[4,32,1152]{2,1,0:T(8,128)S(1)} all-to-all(f32[4,32,1152]{2,1,0:T(8,128)S(1)} %copy.49), channel_id=1, replica_groups=mesh['rows_0'=8,'rows_1'=4,'rows_2'=4,'sub'=2] {'rows_2'}, dimensions={0} | all-to-all | bytes 1179648 | tf_op jit(solution)/shard_map/all_to_all | solution.py:21
  198.6 12.5 %all_to_all.77 = f32[32,1,1152]{2,1,0:T(1,128)S(1)} all-to-all(f32[32,1,1152]{2,1,0:T(1,128)S(1)} %all_to_all.53), channel_id=1, replica_groups=mesh['rows_0'=8,'rows_1'=4,'rows_2'=4,'sub'=2] {'rows_0','rows_1'}, dimensions={0} | all-to-all | bytes 294912 | tf_op jit(solution)/shard_map/all_to_all | solution.py:56
  211.3 12.7 %all_to_all.72 = f32[32,1,1152]{2,1,0:T(1,128)S(1)} all-to-all(f32[32,1,1152]{2,1,0:T(1,128)S(1)} %broadcast_in_dim.92), channel_id=1, replica_groups=mesh['rows_0'=8,'rows_1'=4,'rows_2'=4,'sub'=2] {'rows_0','rows_1'}, dimensions={0} | all-to-all | bytes 294912 | tf_op jit(solution)/shard_map/all_to_all | solution.py:34
  224.9 3.5 all-to-all-start.10
  228.4 2.1 fusion.43
  230.5 5.1 %all-to-all-done.10 = f32[4,32,1152]{2,1,0:T(8,128)S(1)} async-done(((f32[4,32,1152]{2,1,0:T(8,128)}), f32[4,32,1152]{2,1,0:T(8,128)S(1)}, u32[]{:S(2)}, u32[]{:S(2)}) %all-to-all-start.10) | async-done | bytes 589856 | tf_op jit(solution)/shard_map/all_to_all | solution.py:34
  236.4 9.6 %all_to_all.73 = f32[2,192,768]{2,1,0:T(8,128)S(1)} all-to-all(f32[2,192,768]{2,1,0:T(8,128)S(1)} %broadcast_in_dim.96), channel_id=1, replica_groups=mesh['rows_0'=8,'rows_1'=4,'rows_2'=4,'sub'=2] {'sub'}, dimensions={0} | all-to-all | bytes 2359296 | tf_op jit(solution)/shard_map/all_to_all | solution.py:34
  246.8 1.3 copy.75
  250.3 2.1 copy.52
  254.4 11.7 %cholesky.261 = f32[128,128]{1,0:T(8,128)S(1)} custom-call(f32[128,128]{1,0:T(8,128)S(1)} %cholesky.318), custom_call_target="Cholesky" | custom-call | tf_op jit(solution)/shard_map/jit(cholesky)/cholesky | solution.py:118
  266.2 9.8 %custom-call.27 = f32[1,128,128]{1,2,0:T(8,128)S(1)} custom-call(f32[1,128,128]{2,1,0:T(8,128)S(1)} %get-tuple-element.49), custom_call_target="InvertDiagBlocksLowerTriangular" | custom-call | tf_op jit(solution)/shard_map/jit(cholesky)/cholesky | solution.py:118
  277.2 1.2 convolution_subtract_fusion.6
  278.4 11.7 %cholesky.280 = f32[128,128]{1,0:T(8,128)S(1)} custom-call(f32[128,128]{1,0:T(8,128)S(1)} %cholesky.322), custom_call_target="Cholesky" | custom-call | tf_op jit(solution)/shard_map/jit(cholesky)/cholesky | solution.py:118
  291.5 10.2 %custom-call.28 = f32[1,128,128]{1,2,0:T(8,128)S(1)} custom-call(f32[1,128,128]{2,1,0:T(8,128)S(1)} %get-tuple-element.46), custom_call_target="InvertDiagBlocksLowerTriangular" | custom-call | tf_op jit(solution)/shard_map/jit(cholesky)/cholesky | solution.py:118
  303.0 11.7 %cholesky.299 = f32[128,128]{1,0:T(8,128)S(1)} custom-call(f32[128,128]{1,0:T(8,128)S(1)} %convolution_subtract_fusion.8), custom_call_target="Cholesky" | custom-call | tf_op jit(solution)/shard_map/jit(cholesky)/cholesky | solution.py:118
  318.2 8.7 %while.5 = (s32[]{:T(128)}, f32[384,384]{1,0:T(8,128)}, s32[3,2]{0,1:T(2,128)S(1)}, f32[3,128,128]{2,1,0:T(8,128)S(1)}, s32[]{:T(128)}) while((s32[]{:T(128)}, f32[384,384]{1,0:T(8,128)}, s32[3,2]{0,1:T(2,128)S(1)}, f32[3,128,128]{2,1,0:T(8,128)S(1)}, s32[]{:T(128)}) %tuple.53), condition=%wide.while_cond.clone, body=%wide.while_body.clone.sunk | while | flops 2 | bytes 131181 | solution.py:119
  318.8 2.3 bitcast_dynamic-update-slice_fusion.5
  321.7 2.3 bitcast_dynamic-update-slice_fusion.5
  324.6 2.2 bitcast_dynamic-update-slice_fusion.5
  326.9 29.5 %custom-call.29 = f32[3,128,128]{1,2,0:T(8,128)S(1)} custom-call(f32[3,128,128]{2,1,0:T(8,128)S(1)} %get-tuple-element.22), custom_call_target="InvertDiagBlocksLowerTriangular" | custom-call | tf_op jit(solution)/shard_map/triangular_solve/custom-call.2 | solution.py:119
  357.0 1.3 convolution_subtract_fusion.3
  358.4 1.2 fusion.84
  359.6 1.7 convolution_subtract_fusion.2
  361.3 1.3 fusion.82
  362.7 1.3 fusion.26
  363.9 1.3 fusion
  365.3 1.5 fusion.39
  367.8 3.6 gather_fusion
  371.4 3.3 fusion.19
  374.7 1.3 fusion.126
  377.1 1.7 select_reduce_fusion.1
  379.3 2.6 convolution_multiply_fusion.2
  381.9 1.3 convolution_multiply_fusion
  383.3 1.3 convolution_bitcast_fusion
  384.6 1.3 convolution_add_fusion
  385.9 1.3 fusion.1
  387.2 1.5 fusion.41
  389.7 3.6 gather_fusion.1
  394.6 2.1 fusion.14
  396.7 1.3 fusion.122
  400.3 1.3 convolution_add_fusion.1
  (138 shorter events, 36.6 us)
Async XLA Ops:
  0.0 228.4 %copy-start = (f32[384,384]{1,0:T(8,128)S(1)}, f32[384,384]{1,0:T(8,128)}, u32[]{:S(2)}) copy-start(f32[384,384]{1,0:T(8,128)} %param.8) | copy-start | bytes 1769476
  2.6 8.1 %all-to-all-start = ((f32[2,192,384]{2,1,0:T(8,128)}), f32[2,192,384]{2,1,0:T(8,128)S(1)}, u32[]{:S(2)}, u32[]{:S(2)}) async-start(f32[2,192,384]{2,1,0:T(8,128)} %bitcast), calls=%async_computation | async-start | bytes 1179648 | tf_op jit(solution)/shard_map/all_to_all | solution.py:21
  11.0 33.8 %copy-start.17 = (f32[128,384]{1,0:T(8,128)S(1)}, f32[128,384]{1,0:T(8,128)}, u32[]{:S(2)}) copy-start(f32[128,384]{1,0:T(8,128)} %param.7) | copy-start | bytes 589828
  41.0 12.8 %all-to-all-start.3 = ((f32[32,1,576]{2,1,0:T(1,128)}), f32[32,1,576]{2,1,0:T(1,128)S(1)}, u32[]{:S(2)}, u32[]{:S(2)}) async-start(f32[32,1,576]{2,1,0:T(1,128)} %broadcast_in_dim.86), calls=%async_computation.3 | async-start | bytes 163840 | tf_op jit(solution)/shard_map/all_to_all | solution.py:34
  54.6 9.3 %all-to-all-start.4 = ((f32[4,32,576]{2,1,0:T(8,128)}), f32[4,32,576]{2,1,0:T(8,128)S(1)}, u32[]{:S(2)}, u32[]{:S(2)}) async-start(f32[4,32,576]{2,1,0:T(8,128)} %broadcast_in_dim.88), calls=%async_computation.4 | async-start | bytes 655360 | tf_op jit(solution)/shard_map/all_to_all | solution.py:34
  75.7 0.8 copy-start.16
  135.5 92.9 %copy-start.1 = (f32[384,384]{1,0:T(8,128)}, f32[384,384]{1,0:T(8,128)S(1)}, u32[]{:S(2)}) copy-start(f32[384,384]{1,0:T(8,128)S(1)} %get-tuple-element.51) | copy-start | bytes 1769476
  175.3 2.1 copy-start.12
  176.2 1.9 copy-start.7
  176.2 1.9 copy-start.19
  177.4 1.8 copy-start.9
  178.1 8.3 %copy-start.11 = (f32[384,128]{1,0:T(8,128)}, f32[384,128]{1,0:T(8,128)S(1)}, u32[]{:S(2)}) copy-start(f32[384,128]{1,0:T(8,128)S(1)} %fusion.123) | copy-start | bytes 589828
  224.9 10.7 %all-to-all-start.10 = ((f32[4,32,1152]{2,1,0:T(8,128)}), f32[4,32,1152]{2,1,0:T(8,128)S(1)}, u32[]{:S(2)}, u32[]{:S(2)}) async-start(f32[4,32,1152]{2,1,0:T(8,128)} %broadcast_in_dim.94), calls=%async_computation.10 | async-start | bytes 1179648 | tf_op jit(solution)/shard_map/all_to_all | solution.py:34
  253.6 0.8 copy-start.15
  356.4 0.7 copy-start.22
  361.3 2.6 copy-start.14
  362.7 2.6 copy-start.4
  371.4 3.3 copy-start.5
  379.3 2.6 copy-start.3
  383.3 1.3 copy-start.6
  384.5 1.3 copy-start.8
  384.5 1.3 copy-start.10
  385.8 1.3 copy-start.2
  389.7 3.7 copy-start.18
  389.7 3.7 copy-start.20
  393.4 1.2 copy-start.21
  397.9 1.6 copy-start.13

commit v2 on v0

v2 whole, which is shorter than its diff:
```python
import jax
import jax.numpy as jnp
from jax import lax
from jax.experimental import pallas as pl
from jax.experimental.pallas import tpu as pltpu
from jax.sharding import Mesh
from jax.sharding import PartitionSpec as P

SECTIONS = 2
ROWS_SUB = ("rows_0", "rows_1", "rows_2", "sub")


shift_frac = 0.02


def in_blocks(shard, dim, count):
    before, after = (shard.shape[:dim], shard.shape[dim + 1 :])
    return jnp.moveaxis(shard.reshape(*before, count, -1, *after), dim, 0)


def sum_at_owner(shard, axis, dim):
    tiles = in_blocks(shard, dim, lax.axis_size(axis))
    arrived = lax.all_to_all(tiles, axis, split_axis=0, concat_axis=0, tiled=True)
    return arrived.sum(axis=0)


def filled_up(lines, count):
    spare = -lines.shape[0] % count
    if not spare:
        return lines
    return jnp.concatenate([lines, jnp.zeros((spare, *lines.shape[1:]), lines.dtype)])


def sent_to_all(shard, axis):
    count = lax.axis_size(axis)
    return lax.all_to_all(
        jnp.broadcast_to(shard[None], (count, *shard.shape)), axis, 0, 0, tiled=True
    )


def laid_out(tiles, dim):
    dims = list(tiles.shape[1:])
    dims[dim] *= tiles.shape[0]
    return jnp.moveaxis(tiles, 0, dim).reshape(dims)


def gathered_by_axis(shard, axes, dim):
    far, near = axes
    leading = sent_to_all(shard, far)
    tiles = jnp.swapaxes(sent_to_all(leading, near), 0, 1)
    return laid_out(tiles.reshape(-1, *shard.shape), dim)


def sum_in_two_steps(shard, axes, dim):
    far, near = axes
    tiles = in_blocks(shard, dim, lax.axis_size(far))
    nearer = sum_at_owner(tiles, near, dim + 1)
    arrived = lax.all_to_all(nearer, far, split_axis=0, concat_axis=0, tiled=True)
    return arrived.sum(axis=0)


def total_of(shard, axes):
    lines = shard.reshape(-1)
    padded = filled_up(lines, lax.axis_size(axes[0]) * lax.axis_size(axes[1]))
    whole = gathered_by_axis(sum_in_two_steps(padded, axes, 0), axes, 0)
    return lax.slice_in_dim(whole, 0, len(lines)).reshape(shard.shape)


def gathered_copies(shard, axis, dim):
    return laid_out(sent_to_all(shard, axis), dim)


N = 384
BLOCK = 128
GROUP = 8

def mm(left, right, left_dim=1, right_dim=0):
    return lax.dot_general(left, right, (((left_dim,), (right_dim,)), ((), ())),
        precision=lax.Precision.HIGHEST, preferred_element_type=jnp.float32)

def lanes_of(rows, k):
    return jnp.broadcast_to(rows[:, k:k + 1], (GROUP, BLOCK))

def row_of(rows, k):
    return jnp.broadcast_to(rows[k:k + 1, :], (GROUP, BLOCK))

def factor_block(rows):
    count = BLOCK // GROUP
    row = lax.broadcasted_iota(jnp.int32, (GROUP, BLOCK), 0)
    lane = lax.broadcasted_iota(jnp.int32, (GROUP, BLOCK), 1)
    zero = jnp.zeros((GROUP, BLOCK), jnp.float32)
    rows = list(rows)
    inverse = [jnp.where(lane == row + GROUP * q, 1.0, 0.0) for q in range(count)]
    factor = [zero] * count
    heads = [lanes_of(rows[0], k) for k in range(GROUP)]
    for p in range(count):
        first = GROUP * p
        columns = {q: [lanes_of(rows[q], first + k) for k in range(GROUP)] for q in range(p + 1, count)}
        if p + 1 < count:
            next_heads = [lanes_of(rows[p + 1], first + GROUP + k) for k in range(GROUP)]
        panel, side = rows[p], inverse[p]
        panel_rows, side_rows, roots, scalars = [], [], [], {}
        for j in range(GROUP):
            root = lax.rsqrt(row_of(heads[j], j))
            roots.append(root)
            column = heads[j] * root
            factor[p] = jnp.where((lane == first + j) & (row >= j), column, factor[p])
            below = jnp.where(row > j, column, 0.0)
            for k in range(j + 1, GROUP):
                scalars[k, j] = row_of(heads[k], j) * root
                heads[k] = heads[k] - below * scalars[k, j]
            panel_row = row_of(panel, j) * root
            side_row = row_of(side, j) * root
            panel = panel - below * panel_row
            side = jnp.where(row == j, side_row, side - below * side_row)
            panel_rows.append(panel_row)
            side_rows.append(side_row)
        inverse[p] = side
        for q in range(p + 1, count):
            parts = []
            for k in range(GROUP):
                part = columns[q][k]
                for m in range(k):
                    part = part - parts[m] * scalars[k, m]
                part = part * roots[k]
                parts.append(part)
                factor[q] = jnp.where(lane == first + k, part, factor[q])
            if q == p + 1:
                heads = next_heads
                for k in range(GROUP):
                    for m in range(GROUP):
                        heads[k] = heads[k] - parts[m] * row_of(parts[m], k)
            for k in range(GROUP):
                rows[q] = rows[q] - parts[k] * panel_rows[k]
                inverse[q] = inverse[q] - parts[k] * side_rows[k]
    return factor, inverse

def diagonal_mask():
    return lax.broadcasted_iota(jnp.int32, (N, N), 0) == lax.broadcasted_iota(jnp.int32, (N, N), 1)

def factor_whole(gram, rate, l_ref, v_ref, work, small):
    eye = diagonal_mask()
    shift = rate * jnp.sum(jnp.where(eye, gram, 0.0))
    work[...] = jnp.where(eye, gram + shift, gram)
    l_ref[...] = jnp.zeros((N, N), jnp.float32)
    v_ref[...] = jnp.zeros((N, N), jnp.float32)
    row = lax.broadcasted_iota(jnp.int32, (N, BLOCK), 0)

    def step(b, carry):
        start = pl.multiple_of(b * BLOCK, BLOCK)
        here = pl.ds(start, BLOCK)
        factor, inverse = factor_block(
            [work[pl.ds(start + GROUP * q, GROUP), here] for q in range(BLOCK // GROUP)])
        for q in range(BLOCK // GROUP):
            small[pl.ds(GROUP * q, GROUP), :] = inverse[q]
        mixed = mm(l_ref[here, :], v_ref[...])
        inv = small[...]
        v_ref[here, :] = -mm(inv, mixed)
        v_ref[here, here] = inv
        column = jnp.where(row >= start + BLOCK, mm(work[:, here], inv, 1, 1), 0.0)
        l_ref[:, here] = column
        for q in range(BLOCK // GROUP):
            l_ref[pl.ds(start + GROUP * q, GROUP), here] = factor[q]
        work[...] = work[...] - mm(column, column, 1, 1)
        return carry

    lax.fori_loop(0, N // BLOCK, step, 0)


def inner_gram(left, right):
    return lax.dot_general(
        left,
        right,
        (((0,), (0,)), ((), ())),
        precision=lax.Precision.HIGHEST,
        preferred_element_type=jnp.float32,
    )


def summed_gram(partial_value):
    half_rows = sum_at_owner(partial_value, "sub", 0)
    half_rows = total_of(half_rows, (("rows_0", "rows_1"), "rows_2"))
    return gathered_copies(half_rows, "sub", 0)


def upper_mirrored(square):
    row = lax.broadcasted_iota(jnp.int32, (N, N), 0)
    lane = lax.broadcasted_iota(jnp.int32, (N, N), 1)
    upper = jnp.where(lane > row, square, 0.0)
    return upper + upper.T + jnp.where(lane == row, square, 0.0)


def upper_part(square):
    row = lax.broadcasted_iota(jnp.int32, (N, N), 0)
    lane = lax.broadcasted_iota(jnp.int32, (N, N), 1)
    return jnp.where(lane >= row, square, 0.0)


def gram_cotangent(total_grad, lower_fac, lower_inv, rate):
    mirrored = upper_mirrored(mm(upper_part(total_grad), lower_fac))
    weight = 0.5 * mm(lower_inv.T, mm(mirrored, lower_inv))
    eye = diagonal_mask()
    shift = rate * jnp.sum(jnp.where(eye, weight, 0.0))
    return jnp.where(eye, weight + shift, weight)


def first_kernel(gram, a, g, grad_factor, l1, v1, q1, b2, both, work, small):
    factor_whole(gram[...], shift_frac / N, l1, v1, work, small)
    middle = mm(a[...], v1[...], 1, 1)
    q1[...] = middle
    both[:, :N] = mm(middle, middle, 0, 0)
    both[:, N:] = mm(middle, g[...], 0, 0)
    b2[...] = mm(grad_factor[...], l1[...])


def second_kernel(both, a, g, grad_factor, l1, v1, q1, b2, out, l2, v2, work, small):
    rate = shift_frac / N
    gram, crossed = both[:, :N], both[:, N:]
    factor_whole(gram, rate, l2, v2, work, small)
    fac2, inv2 = l2[...], v2[...]
    weight2 = gram_cotangent(b2[...] - mm(mm(inv2, crossed), inv2), fac2, inv2, rate)
    inv1 = v1[...]
    cross1 = mm(crossed, inv2) + 2.0 * mm(gram, weight2)
    weight1 = gram_cotangent(mm(fac2, grad_factor[...]) - mm(cross1, inv1), l1[...], inv1, rate)
    middle_grad = mm(g[...], inv2) + 2.0 * mm(q1[...], weight2)
    out[...] = mm(middle_grad, inv1) + 2.0 * mm(a[...], weight1)


def local_call(kernel, outs, scratch, name, *operands):
    vmem = pl.BlockSpec(memory_space=pltpu.VMEM)
    return pl.pallas_call(
        kernel,
        out_shape=[jax.ShapeDtypeStruct(shape, jnp.float32) for shape in outs],
        in_specs=[vmem] * len(operands),
        out_specs=[vmem] * len(outs),
        scratch_shapes=[pltpu.VMEM(shape, jnp.float32) for shape in scratch],
        compiler_params=pltpu.CompilerParams(vmem_limit_bytes=48 * 1024 * 1024),
        name=name,
    )(*operands)


def per_device(matrix, grad_out, grad_factor):
    square, rows = (N, N), matrix.shape
    first = summed_gram(inner_gram(matrix, matrix))
    l1, v1, q1, b2, both = local_call(
        first_kernel, [square, square, rows, square, (N, 2 * N)], [square, (BLOCK, BLOCK)],
        "first", first, matrix, grad_out, grad_factor)
    both = summed_gram(both)
    return local_call(
        second_kernel, [rows], [square, square, square, (BLOCK, BLOCK)],
        "second", both, matrix, grad_out, grad_factor, l1, v1, q1, b2)[0]


def solution(mesh):
    torus = Mesh(
        mesh.devices.reshape(8, 4, 4, mesh.shape["sub"]), ("rows_0", "rows_1", "rows_2", "sub")
    )
    in_specs = (P(ROWS_SUB, None), P(ROWS_SUB, None), P())
    out_specs = P(ROWS_SUB, None)
    return jax.shard_map(
        per_device, mesh=torus, in_specs=in_specs, out_specs=out_specs, check_vma=False
    )
```

time: 526 us -> 191 us (0.36)
  other arithmetic: 184 us -> 3.16 us
  Pallas kernels: 0 us -> 52 us
  local copies, waits for them, and re-layouts: 51.9 us -> 6.14 us
  matrix products: 45.1 us -> 1.69 us
  blocking collectives: 170 us -> 127 us
  waiting for transfers between devices: 33.7 us -> 0 us
  starting transfers between devices: 29 us -> 0 us
  between operations: 7.28 us -> 0.15 us
    another operation x26 -> x0, other arithmetic: 173 us -> none  [the longest x21 113 us: per_device(): lower_fac = jnp.linalg.cholesky(summed + shift_val * identity)]
    pallas_call x0 -> x2, Pallas kernels: none -> 52 us  [local_call(): pl.pallas_call(kernel, out_shape=[jax.ShapeDtypeStruct(shape, jnp.float32...]
    all_to_all x5 -> x0, waiting for transfers between devices: 33.7 us -> none  [the longest x4 32.2 us: sent_to_all(): lax.all_to_all(jnp.broadcast_to(shard[None], (count, *shard.shape)), axis...]
    all_to_all x5 -> x0, starting transfers between devices: 29 us -> none  [the longest x4 22.3 us: sent_to_all(): lax.all_to_all(jnp.broadcast_to(shard[None], (count, *shard.shape)), axis...]
    dot_general x16 -> x0, matrix products: 26.7 us -> none  [full_dot(): jnp.dot(left, right, precision=lax.Precision.HIGHEST, preferred_element_t...]
    all_to_all x4 -> x2, blocking collectives: 55.8 us -> 32.6 us  [sum_in_two_steps(): lax.all_to_all(nearer, far, split_axis=0, concat_axis=0, tiled=True)]
    all_to_all x5 -> x4, blocking collectives: 52.1 us -> 33.7 us  [sum_at_owner(): lax.all_to_all(tiles, axis, split_axis=0, concat_axis=0, tiled=True)]
    another operation x29 -> x0, local copies, waits for them, and re-layouts: 18.3 us -> none  [the longest x21 14.7 us: per_device(): lax.linalg.triangular_solve(lower_fac, identity, left_side=True, lower=True)]
  transfers between devices with their start and end apart: 5 -> 0, of which waited for: 5 -> 0; matrix products, arithmetic and copies ran while one was open for 1% -> 0% of each run, Pallas kernels for 0% -> 0%
where the time goes in v2:
time: 191 us; the launch traced here: 190 us
  blocking collectives  127 us (66%)
  Pallas kernels  52 us (27%)
  local copies, waits for them, and re-layouts  6.14 us (3%)
  other arithmetic  3.16 us (2%)
    all_to_all x6, blocking collectives, sent_to_all(): lax.all_to_all(jnp.broadcast_to(shard[None], (count, *shard.shape)), axis...  61.1 us
    pallas_call x2, Pallas kernels, local_call(): pl.pallas_call(kernel, out_shape=[jax.ShapeDtypeStruct(shape, jnp.float32...  52 us
    all_to_all x4, blocking collectives, sum_at_owner(): lax.all_to_all(tiles, axis, split_axis=0, concat_axis=0, tiled=True)  33.7 us
    all_to_all x2, blocking collectives, sum_in_two_steps(): lax.all_to_all(nearer, far, split_axis=0, concat_axis=0, tiled=True)  32.6 us

profile of v2, /device:TPU:1, one launch (start us, length us, event | category | flops | bytes accessed | tf_op | source)
XLA Modules:
  0.0 190.5 jit_solution(261489152021211758)
XLA Ops:
  0.0 1.7 fusion
  1.7 7.0 %all_to_all.70 = f32[2,192,384]{2,1,0:T(8,128)S(1)} all-to-all(f32[2,192,384]{2,1,0:T(8,128)S(1)} %bitcast.21), channel_id=1, replica_groups=mesh['rows_0'=8,'rows_1'=4,'rows_2'=4,'sub'=2] {'sub'}, dimensions={0} | all-to-all | bytes 1179648 | tf_op jit(solution)/shard_map/all_to_all | solution.py:23
  8.8 0.3 reshape_reshape_reshape.6
  9.1 9.2 %all_to_all.71 = f32[4,32,576]{2,1,0:T(8,128)S(1)} all-to-all(f32[4,32,576]{2,1,0:T(8,128)S(1)} %copy.4), channel_id=1, replica_groups=mesh['rows_0'=8,'rows_1'=4,'rows_2'=4,'sub'=2] {'rows_2'}, dimensions={0} | all-to-all | bytes 589824 | tf_op jit(solution)/shard_map/all_to_all | solution.py:23
  18.3 0.1 all_to_all.46
  18.3 19.8 %all_to_all.72 = f32[32,1,576]{2,1,0:T(1,128)S(1)} all-to-all(f32[32,1,576]{2,1,0:T(1,128)S(1)} %all_to_all.46), channel_id=1, replica_groups=mesh['rows_0'=8,'rows_1'=4,'rows_2'=4,'sub'=2] {'rows_0','rows_1'}, dimensions={0} | all-to-all | bytes 147456 | tf_op jit(solution)/shard_map/all_to_all | solution.py:58
  38.1 0.1 reduce_sum.56
  38.3 12.0 %all_to_all.73 = f32[32,1,576]{2,1,0:T(1,128)S(1)} all-to-all(f32[32,1,576]{2,1,0:T(1,128)S(1)} %broadcast_in_dim.20), channel_id=1, replica_groups=mesh['rows_0'=8,'rows_1'=4,'rows_2'=4,'sub'=2] {'rows_0','rows_1'}, dimensions={0} | all-to-all | bytes 147456 | tf_op jit(solution)/shard_map/all_to_all | solution.py:36
  50.3 8.3 %all_to_all.74 = f32[4,32,576]{2,1,0:T(8,128)S(1)} all-to-all(f32[4,32,576]{2,1,0:T(8,128)S(1)} %broadcast_in_dim.44), channel_id=1, replica_groups=mesh['rows_0'=8,'rows_1'=4,'rows_2'=4,'sub'=2] {'rows_2'}, dimensions={0} | all-to-all | bytes 589824 | tf_op jit(solution)/shard_map/all_to_all | solution.py:36
  58.6 0.2 copy.5
  58.8 0.3 broadcast_in_dim.45
  59.1 0.0 copy-start
  59.1 0.0 copy-start.1
  59.1 0.0 copy-start.2
  59.2 9.2 %all_to_all.75 = f32[2,192,384]{2,1,0:T(8,128)S(1)} all-to-all(f32[2,192,384]{2,1,0:T(8,128)S(1)} %broadcast_in_dim.46), channel_id=1, replica_groups=mesh['rows_0'=8,'rows_1'=4,'rows_2'=4,'sub'=2] {'sub'}, dimensions={0} | all-to-all | bytes 1179648 | tf_op jit(solution)/shard_map/all_to_all | solution.py:36
  68.3 0.0 copy-done
  68.3 0.0 copy-done.1
  68.3 0.0 copy-done.2
  68.3 18.5 %first.1 = (f32[384,384]{1,0:T(8,128)S(1)}, f32[384,384]{1,0:T(8,128)S(1)}, f32[128,384]{1,0:T(8,128)S(1)}, f32[384,384]{1,0:T(8,128)S(1)}, f32[384,768]{1,0:T(8,128)S(1)}) custom-call(f32[384,384]{1,0:T(8,128)S(1)} %bitcast.17, f32[128,384]{1,0:T(8,128)S(1)} %copy-done, f32[128,384]{1,0:T(8,128)S(1)} %copy-done.2, f32[384,384]{1,0:T(8,128)S(1)} %copy-done.1), custom_call_target="tpu_custom_call" | custom-call | tf_op jit(solution)/shard_map/first/pallas_call | solution.py:231
  86.8 5.5 %all_to_all.76 = f32[2,192,768]{2,1,0:T(8,128)} all-to-all(f32[2,192,768]{2,1,0:T(8,128)S(1)} %bitcast.18), channel_id=1, replica_groups=mesh['rows_0'=8,'rows_1'=4,'rows_2'=4,'sub'=2] {'sub'}, dimensions={0} | all-to-all | bytes 2359296 | tf_op jit(solution)/shard_map/all_to_all | solution.py:23
  92.3 2.3 %reduce_sum.57 = f32[192,768]{1,0:T(8,128)} reduce(f32[2,192,768]{2,1,0:T(8,128)} %all_to_all.76, f32[]{:T(128)} %constant.0.clone.1), dimensions={0}, to_apply=%region_3.0 | reduce | flops 147456 | bytes 1769476 | tf_op jit(solution)/shard_map/reduce_sum | solution.py:24
  94.5 1.3 reshape_reshape_reshape.7
  95.9 12.0 %all_to_all.77 = f32[4,32,1152]{2,1,0:T(8,128)S(1)} all-to-all(f32[4,32,1152]{2,1,0:T(8,128)S(1)} %copy.6), channel_id=1, replica_groups=mesh['rows_0'=8,'rows_1'=4,'rows_2'=4,'sub'=2] {'rows_2'}, dimensions={0} | all-to-all | bytes 1179648 | tf_op jit(solution)/shard_map/all_to_all | solution.py:23
  107.9 0.7 reduce_sum.58
  108.6 1.0 all_to_all.53
  109.6 12.7 %all_to_all.78 = f32[32,1,1152]{2,1,0:T(1,128)S(1)} all-to-all(f32[32,1,1152]{2,1,0:T(1,128)S(1)} %all_to_all.53), channel_id=1, replica_groups=mesh['rows_0'=8,'rows_1'=4,'rows_2'=4,'sub'=2] {'rows_0','rows_1'}, dimensions={0} | all-to-all | bytes 294912 | tf_op jit(solution)/shard_map/all_to_all | solution.py:58
  122.4 0.1 reduce_sum.59
  122.5 0.1 broadcast_in_dim.47
  122.6 12.7 %all_to_all.79 = f32[32,1,1152]{2,1,0:T(1,128)S(1)} all-to-all(f32[32,1,1152]{2,1,0:T(1,128)S(1)} %broadcast_in_dim.47), channel_id=1, replica_groups=mesh['rows_0'=8,'rows_1'=4,'rows_2'=4,'sub'=2] {'rows_0','rows_1'}, dimensions={0} | all-to-all | bytes 294912 | tf_op jit(solution)/shard_map/all_to_all | solution.py:36
  135.3 9.7 %all_to_all.80 = f32[4,32,1152]{2,1,0:T(8,128)S(1)} all-to-all(f32[4,32,1152]{2,1,0:T(8,128)S(1)} %broadcast_in_dim.49), channel_id=1, replica_groups=mesh['rows_0'=8,'rows_1'=4,'rows_2'=4,'sub'=2] {'rows_2'}, dimensions={0} | all-to-all | bytes 1179648 | tf_op jit(solution)/shard_map/all_to_all | solution.py:36
  145.0 1.2 copy.7
  146.2 1.4 broadcast_in_dim.50
  147.5 0.1 broadcast_in_dim.51
  147.6 9.3 %all_to_all.81 = f32[2,192,768]{2,1,0:T(8,128)S(1)} all-to-all(f32[2,192,768]{2,1,0:T(8,128)S(1)} %broadcast_in_dim.51), channel_id=1, replica_groups=mesh['rows_0'=8,'rows_1'=4,'rows_2'=4,'sub'=2] {'sub'}, dimensions={0} | all-to-all | bytes 2359296 | tf_op jit(solution)/shard_map/all_to_all | solution.py:36
  157.0 33.5 %second.1 = f32[128,384]{1,0:T(8,128)} custom-call(f32[384,768]{1,0:T(8,128)S(1)} %bitcast.16, f32[128,384]{1,0:T(8,128)S(1)} %copy-done, f32[128,384]{1,0:T(8,128)S(1)} %copy-done.2, f32[384,384]{1,0:T(8,128)S(1)} %copy-done.1, f32[384,384]{1,0:T(8,128)S(1)} %get-tuple-element.11.l1, f32[384,384]{1,0:T(8,128)S(1)} %get-tuple-element.12.v1, ...), custom_call_target="tpu_custom_call" | custom-call | tf_op jit(solution)/shard_map/second/pallas_call | solution.py:231
  (10 shorter events, 0.3 us)
Async XLA Ops:
  59.1 9.2 %copy-start = (f32[128,384]{1,0:T(8,128)S(1)}, f32[128,384]{1,0:T(8,128)}, u32[]{:S(2)}) copy-start(f32[128,384]{1,0:T(8,128)} %a.3) | copy-start | bytes 589828
  59.1 9.2 %copy-start.1 = (f32[384,384]{1,0:T(8,128)S(1)}, f32[384,384]{1,0:T(8,128)}, u32[]{:S(2)}) copy-start(f32[384,384]{1,0:T(8,128)} %grad_factor.3) | copy-start | bytes 1769476
  59.1 9.2 %copy-start.2 = (f32[128,384]{1,0:T(8,128)S(1)}, f32[128,384]{1,0:T(8,128)}, u32[]{:S(2)}) copy-start(f32[128,384]{1,0:T(8,128)} %g.3) | copy-start | bytes 589828

commit v3 on v2

--- a/solution.py
+++ b/solution.py
@@ -6,70 +6,9 @@
 from jax.sharding import Mesh
 from jax.sharding import PartitionSpec as P
 
-SECTIONS = 2
-ROWS_SUB = ("rows_0", "rows_1", "rows_2", "sub")
-
-
+AXES = ("z", "y", "x", "core")
+DEEP, SIDE, PLANE = 8, 4, 16
 shift_frac = 0.02
-
-
-def in_blocks(shard, dim, count):
-    before, after = (shard.shape[:dim], shard.shape[dim + 1 :])
-    return jnp.moveaxis(shard.reshape(*before, count, -1, *after), dim, 0)
-
-
-def sum_at_owner(shard, axis, dim):
-    tiles = in_blocks(shard, dim, lax.axis_size(axis))
-    arrived = lax.all_to_all(tiles, axis, split_axis=0, concat_axis=0, tiled=True)
-    return arrived.sum(axis=0)
-
-
-def filled_up(lines, count):
-    spare = -lines.shape[0] % count
-    if not spare:
-        return lines
-    return jnp.concatenate([lines, jnp.zeros((spare, *lines.shape[1:]), lines.dtype)])
-
-
-def sent_to_all(shard, axis):
-    count = lax.axis_size(axis)
-    return lax.all_to_all(
-        jnp.broadcast_to(shard[None], (count, *shard.shape)), axis, 0, 0, tiled=True
-    )
-
-
-def laid_out(tiles, dim):
-    dims = list(tiles.shape[1:])
-    dims[dim] *= tiles.shape[0]
-    return jnp.moveaxis(tiles, 0, dim).reshape(dims)
-
-
-def gathered_by_axis(shard, axes, dim):
-    far, near = axes
-    leading = sent_to_all(shard, far)
-    tiles = jnp.swapaxes(sent_to_all(leading, near), 0, 1)
-    return laid_out(tiles.reshape(-1, *shard.shape), dim)
-
-
-def sum_in_two_steps(shard, axes, dim):
-    far, near = axes
-    tiles = in_blocks(shard, dim, lax.axis_size(far))
-    nearer = sum_at_owner(tiles, near, dim + 1)
-    arrived = lax.all_to_all(nearer, far, split_axis=0, concat_axis=0, tiled=True)
-    return arrived.sum(axis=0)
-
-
-def total_of(shard, axes):
-    lines = shard.reshape(-1)
-    padded = filled_up(lines, lax.axis_size(axes[0]) * lax.axis_size(axes[1]))
-    whole = gathered_by_axis(sum_in_two_steps(padded, axes, 0), axes, 0)
-    return lax.slice_in_dim(whole, 0, len(lines)).reshape(shard.shape)
-
-
-def gathered_copies(shard, axis, dim):
-    return laid_out(sent_to_all(shard, axis), dim)
-
-
 N = 384
 BLOCK = 128
 GROUP = 8
@@ -167,20 +106,188 @@
     lax.fori_loop(0, N // BLOCK, step, 0)
 
 
-def inner_gram(left, right):
-    return lax.dot_general(
-        left,
-        right,
-        (((0,), (0,)), ((), ())),
-        precision=lax.Precision.HIGHEST,
-        preferred_element_type=jnp.float32,
+def hops(step):
+    return sum(min(part, SIDE - part) for part in (step // SIDE, step % SIDE))
+
+
+PLANE_STEPS = sorted(range(1, PLANE), key=hops, reverse=True)
+DEEP_STEPS = sorted(range(1, DEEP), key=lambda step: min(step, DEEP - step), reverse=True)
+
+
+def position():
+    return tuple(lax.axis_index(name) for name in AXES)
+
+
+def plane_peer(step, sign):
+    z, y, x, core = position()
+    return (
+        z,
+        lax.rem(y + sign * (step // SIDE) + SIDE, SIDE),
+        lax.rem(x + sign * (step % SIDE) + SIDE, SIDE),
+        core,
     )
 
 
-def summed_gram(partial_value):
-    half_rows = sum_at_owner(partial_value, "sub", 0)
-    half_rows = total_of(half_rows, (("rows_0", "rows_1"), "rows_2"))
-    return gathered_copies(half_rows, "sub", 0)
+def deep_peer(step, sign):
+    z, y, x, core = position()
+    return (lax.rem(z + sign * step + DEEP, DEEP), y, x, core)
+
+
+def core_peer():
+    z, y, x, core = position()
+    return (z, y, x, 1 - core)
+
+
+def greet():
+    barrier = pltpu.get_barrier_semaphore()
+    peers = [core_peer()] + [plane_peer(s, 1) for s in PLANE_STEPS] + [deep_peer(s, 1) for s in DEEP_STEPS]
+    for peer in peers:
+        pl.semaphore_signal(barrier, inc=1, device_id=peer, device_id_type=pl.DeviceIdType.MESH)
+
+
+def meet():
+    pl.semaphore_wait(pltpu.get_barrier_semaphore(), DEEP + PLANE - 1)
+
+
+def comm_scratch(rows):
+    chunk = rows // (2 * PLANE)
+    dma = pltpu.SemaphoreType.DMA
+    return [
+        pltpu.VMEM((rows, BLOCK), jnp.float32),
+        pltpu.VMEM((rows // 2, BLOCK), jnp.float32),
+        pltpu.VMEM((rows // 2, BLOCK), jnp.float32),
+        pltpu.VMEM((PLANE, chunk, BLOCK), jnp.float32),
+        pltpu.VMEM((DEEP, chunk, BLOCK), jnp.float32),
+        pltpu.VMEM((rows, BLOCK), jnp.float32),
+        dma((2, 2)),
+        dma((2, PLANE)),
+        dma((2, DEEP)),
+        dma((2, PLANE)),
+        dma((2, 2)),
+    ]
+
+
+def sum_over_devices(packed, half, got, arrived, deep, total, sem_core, sem_plane, sem_deep, sem_out, sem_last, between=None):
+    rows = packed.shape[0]
+    chunk = rows // (2 * PLANE)
+    z, y, x, core = position()
+    place = y * SIDE + x
+    sent = []
+
+    def send(src, dst, send_sem, recv_sem, peer):
+        copy = pltpu.make_async_remote_copy(
+            src_ref=src, dst_ref=dst, send_sem=send_sem, recv_sem=recv_sem,
+            device_id=peer, device_id_type=pl.DeviceIdType.MESH)
+        copy.start()
+        sent.append(copy)
+        return copy
+
+    def part(ref, index, size):
+        return ref.at[pl.ds(pl.multiple_of(index * size, size), size), :]
+
+    send(part(packed, 1 - core, rows // 2), got, sem_core.at[0, 0], sem_core.at[1, 0], core_peer()).wait_recv()
+    half[...] = got[...] + packed[pl.ds(pl.multiple_of(core * (rows // 2), rows // 2), rows // 2), :]
+
+    copies = []
+    for step in PLANE_STEPS:
+        peer = plane_peer(step, 1)
+        copies.append(send(part(half, peer[1] * SIDE + peer[2], chunk), arrived.at[step],
+                           sem_plane.at[0, step], sem_plane.at[1, step], peer))
+    if between is not None:
+        between()
+    own = half[pl.ds(pl.multiple_of(place * chunk, chunk), chunk), :]
+    for copy, step in zip(copies, PLANE_STEPS):
+        copy.wait_recv()
+    for step in range(1, PLANE):
+        own = own + arrived[step]
+    deep[z] = own
+
+    copies = []
+    for step in DEEP_STEPS:
+        copies.append(send(deep.at[z], deep.at[z], sem_deep.at[0, step], sem_deep.at[1, step], deep_peer(step, 1)))
+    for step in DEEP_STEPS:
+        source = deep_peer(step, -1)[0]
+        pltpu.make_async_remote_copy(
+            src_ref=deep.at[source], dst_ref=deep.at[source], send_sem=sem_deep.at[0, step],
+            recv_sem=sem_deep.at[1, step], device_id=deep_peer(step, -1),
+            device_id_type=pl.DeviceIdType.MESH).wait_recv()
+    whole = deep[0]
+    for index in range(1, DEEP):
+        whole = whole + deep[index]
+    mine = core * PLANE + place
+    total[pl.ds(pl.multiple_of(mine * chunk, chunk), chunk), :] = whole
+
+    for step in PLANE_STEPS:
+        spot = part(total, mine, chunk)
+        send(spot, spot, sem_out.at[0, step], sem_out.at[1, step], plane_peer(step, 1))
+    for step in PLANE_STEPS:
+        peer = plane_peer(step, -1)
+        spot = part(total, core * PLANE + peer[1] * SIDE + peer[2], chunk)
+        pltpu.make_async_remote_copy(
+            src_ref=spot, dst_ref=spot, send_sem=sem_out.at[0, step], recv_sem=sem_out.at[1, step],
+            device_id=peer, device_id_type=pl.DeviceIdType.MESH).wait_recv()
+
+    spot = part(total, core, rows // 2)
+    send(spot, spot, sem_last.at[0, 0], sem_last.at[1, 0], core_peer())
+    spot = part(total, 1 - core, rows // 2)
+    pltpu.make_async_remote_copy(
+        src_ref=spot, dst_ref=spot, send_sem=sem_last.at[0, 0], recv_sem=sem_last.at[1, 0],
+        device_id=core_peer(), device_id_type=pl.DeviceIdType.MESH).wait_recv()
+    for copy in sent:
+        copy.wait_send()
+
+
+LOWER = [(i, j) for i in range(3) for j in range(i + 1)]
+EVERY = [(i, j) for i in range(3) for j in range(3)]
+
+
+def block_of(ref, i, j):
+    return ref.at[pl.ds(i * BLOCK, BLOCK), pl.ds(j * BLOCK, BLOCK)]
+
+
+def packed_rows(index):
+    return pl.ds(index * BLOCK, BLOCK)
+
+
+def unpack_symmetric(total, out):
+    for index, (i, j) in enumerate(LOWER):
+        value = total[packed_rows(index), :]
+        block_of(out, i, j)[...] = value
+        if i != j:
+            block_of(out, j, i)[...] = value.T
+
+
+def first_sum_kernel(a, gram, packed, *scratch):
+    greet()
+    local = mm(a[...], a[...], 0, 0)
+    for index, (i, j) in enumerate(LOWER):
+        packed[packed_rows(index), :] = local[i * BLOCK:(i + 1) * BLOCK, j * BLOCK:(j + 1) * BLOCK]
+    meet()
+    sum_over_devices(packed, *scratch)
+    unpack_symmetric(scratch[4], gram)
+
+
+def second_sum_kernel(a, g, grad_factor, l1, v1, q1, b2, gram, crossed, packed, *scratch):
+    greet()
+    middle = mm(a[...], v1[...], 1, 1)
+    q1[...] = middle
+    local = mm(middle, middle, 0, 0)
+    for index, (i, j) in enumerate(LOWER):
+        packed[packed_rows(index), :] = local[i * BLOCK:(i + 1) * BLOCK, j * BLOCK:(j + 1) * BLOCK]
+    local = mm(middle, g[...], 0, 0)
+    for index, (i, j) in enumerate(EVERY):
+        packed[packed_rows(len(LOWER) + index), :] = local[i * BLOCK:(i + 1) * BLOCK, j * BLOCK:(j + 1) * BLOCK]
+    packed[packed_rows(len(LOWER) + len(EVERY)), :] = jnp.zeros((BLOCK, BLOCK), jnp.float32)
+    meet()
+
+    def between():
+        b2[...] = mm(grad_factor[...], l1[...])
+
+    sum_over_devices(packed, *scratch, between=between)
+    total = scratch[4]
+    unpack_symmetric(total, gram)
+    for index, (i, j) in enumerate(EVERY):
+        block_of(crossed, i, j)[...] = total[packed_rows(len(LOWER) + index), :]
 
 
 def upper_mirrored(square):
@@ -204,18 +311,13 @@
     return jnp.where(eye, weight + shift, weight)
 
 
-def first_kernel(gram, a, g, grad_factor, l1, v1, q1, b2, both, work, small):
+def first_kernel(gram, l1, v1, work, small):
     factor_whole(gram[...], shift_frac / N, l1, v1, work, small)
-    middle = mm(a[...], v1[...], 1, 1)
-    q1[...] = middle
-    both[:, :N] = mm(middle, middle, 0, 0)
-    both[:, N:] = mm(middle, g[...], 0, 0)
-    b2[...] = mm(grad_factor[...], l1[...])
-
-
-def second_kernel(both, a, g, grad_factor, l1, v1, q1, b2, out, l2, v2, work, small):
+
+
+def second_kernel(gram_ref, crossed_ref, a, g, grad_factor, l1, v1, q1, b2, out, l2, v2, work, small):
     rate = shift_frac / N
-    gram, crossed = both[:, :N], both[:, N:]
+    gram, crossed = gram_ref[...], crossed_ref[...]
     factor_whole(gram, rate, l2, v2, work, small)
     fac2, inv2 = l2[...], v2[...]
     weight2 = gram_cotangent(b2[...] - mm(mm(inv2, crossed), inv2), fac2, inv2, rate)
@@ -226,37 +328,38 @@
     out[...] = mm(middle_grad, inv1) + 2.0 * mm(a[...], weight1)
 
 
-def local_call(kernel, outs, scratch, name, *operands):
+def call(kernel, outs, scratch, name, *operands, **params):
     vmem = pl.BlockSpec(memory_space=pltpu.VMEM)
     return pl.pallas_call(
         kernel,
         out_shape=[jax.ShapeDtypeStruct(shape, jnp.float32) for shape in outs],
         in_specs=[vmem] * len(operands),
         out_specs=[vmem] * len(outs),
-        scratch_shapes=[pltpu.VMEM(shape, jnp.float32) for shape in scratch],
-        compiler_params=pltpu.CompilerParams(vmem_limit_bytes=48 * 1024 * 1024),
+        scratch_shapes=scratch,
+        compiler_params=pltpu.CompilerParams(vmem_limit_bytes=48 * 1024 * 1024, **params),
         name=name,
     )(*operands)
 
 
 def per_device(matrix, grad_out, grad_factor):
     square, rows = (N, N), matrix.shape
-    first = summed_gram(inner_gram(matrix, matrix))
-    l1, v1, q1, b2, both = local_call(
-        first_kernel, [square, square, rows, square, (N, 2 * N)], [square, (BLOCK, BLOCK)],
-        "first", first, matrix, grad_out, grad_factor)
-    both = summed_gram(both)
-    return local_call(
-        second_kernel, [rows], [square, square, square, (BLOCK, BLOCK)],
-        "second", both, matrix, grad_out, grad_factor, l1, v1, q1, b2)[0]
+    work = [pltpu.VMEM(square, jnp.float32), pltpu.VMEM((BLOCK, BLOCK), jnp.float32)]
+    (gram1,) = call(first_sum_kernel, [square], comm_scratch(len(LOWER) * BLOCK), "sum1", matrix,
+                    collective_id=0, has_side_effects=True)
+    l1, v1 = call(first_kernel, [square] * 2, work, "first", gram1)
+    q1, b2, gram2, crossed = call(
+        second_sum_kernel, [rows, square, square, square], comm_scratch(PLANE * BLOCK), "sum2",
+        matrix, grad_out, grad_factor, l1, v1, collective_id=1, has_side_effects=True)
+    return call(second_kernel, [rows], [pltpu.VMEM(square, jnp.float32)] * 2 + work, "second",
+                gram2, crossed, matrix, grad_out, grad_factor, l1, v1, q1, b2)[0]
 
 
 def solution(mesh):
-    torus = Mesh(
-        mesh.devices.reshape(8, 4, 4, mesh.shape["sub"]), ("rows_0", "rows_1", "rows_2", "sub")
+    torus = Mesh(mesh.devices.reshape(DEEP, SIDE, SIDE, 2), AXES)
+    return jax.shard_map(
+        per_device,
+        mesh=torus,
+        in_specs=(P(AXES, None), P(AXES, None), P()),
+        out_specs=P(AXES, None),
+        check_vma=False,
     )
-    in_specs = (P(ROWS_SUB, None), P(ROWS_SUB, None), P())
-    out_specs = P(ROWS_SUB, None)
-    return jax.shard_map(
-        per_device, mesh=torus, in_specs=in_specs, out_specs=out_specs, check_vma=False
-    )

time: 191 us -> 110 us (0.58)
  blocking collectives: 127 us -> 0 us
  Pallas kernels: 52 us -> 109 us
  local copies, waits for them, and re-layouts: 6.14 us -> 1 us
  other arithmetic: 3.16 us -> 0 us
    all_to_all x12 -> x0, blocking collectives: 127 us -> none  [the longest x6 61.1 us: sent_to_all(): lax.all_to_all(jnp.broadcast_to(shard[None], (count, *shard.shape)), axis...]
    pallas_call x2 -> x4, Pallas kernels: 52 us -> 109 us  [call(): pl.pallas_call(kernel, out_shape=[jax.ShapeDtypeStruct(shape, jnp.float32...]
    reduce_sum x6 -> x0, other arithmetic: 3.16 us -> none  [the longest x4 2.99 us: sum_at_owner(): return arrived.sum(axis=0)]
    broadcast_in_dim x8 -> x0, local copies, waits for them, and re-layouts: 1.97 us -> none  [sent_to_all(): jnp.broadcast_to(shard[None], (count, *shard.shape))]
where the time goes in v3:
time: 110 us
  Pallas kernels  109 us (99%)
    pallas_call x4, Pallas kernels, call(): pl.pallas_call(kernel, out_shape=[jax.ShapeDtypeStruct(shape, jnp.float32...  109 us

profile of v3, /device:TPU:1, one launch (start us, length us, event | category | flops | bytes accessed | tf_op | source)
XLA Modules:
  0.0 110.4 jit_solution(7227073851744316125)
XLA Ops:
  0.0 0.0 copy-start
  0.0 0.0 copy-start.1
  0.0 1.0 copy-done.1
  1.0 29.6 %sum1.1.gram = f32[384,384]{1,0:T(8,128)S(1)} custom-call(f32[128,384]{1,0:T(8,128)S(1)} %copy-done.1), custom_call_target="tpu_custom_call" | custom-call | tf_op jit(solution)/shard_map/sum1/pallas_call | solution.py:333
  30.6 0.0 copy-start.2
  30.6 15.4 %first.1 = (f32[384,384]{1,0:T(8,128)S(1)}, f32[384,384]{1,0:T(8,128)S(1)}) custom-call(f32[384,384]{1,0:T(8,128)S(1)} %sum1.1.gram), custom_call_target="tpu_custom_call" | custom-call | tf_op jit(solution)/shard_map/first/pallas_call | solution.py:333
  46.0 0.0 copy-done
  46.0 0.0 copy-done.2
  46.1 30.9 %sum2.1 = (f32[128,384]{1,0:T(8,128)S(1)}, f32[384,384]{1,0:T(8,128)S(1)}, f32[384,384]{1,0:T(8,128)S(1)}, f32[384,384]{1,0:T(8,128)S(1)}) custom-call(f32[128,384]{1,0:T(8,128)S(1)} %copy-done.1, f32[128,384]{1,0:T(8,128)S(1)} %copy-done.2, f32[384,384]{1,0:T(8,128)S(1)} %copy-done, f32[384,384]{1,0:T(8,128)S(1)} %get-tuple-element.11.l1, ...), custom_call_target="tpu_custom_call" | custom-call | tf_op jit(solution)/shard_map/sum2/pallas_call | solution.py:333
  76.9 33.5 %second.1 = f32[128,384]{1,0:T(8,128)} custom-call(f32[384,384]{1,0:T(8,128)S(1)} %get-tuple-element.13.gram_ref, f32[384,384]{1,0:T(8,128)S(1)} %get-tuple-element.14.crossed_ref, f32[128,384]{1,0:T(8,128)S(1)} %copy-done.1, f32[128,384]{1,0:T(8,128)S(1)} %copy-done.2, f32[384,384]{1,0:T(8,128)S(1)} %copy-done, f32[384,384]{1,0:T(8,128)S(1)} %get-tuple-element.11.l1, ...), custom_call_target="tpu_custom_call" | custom-call | tf_op jit(solution)/shard_map/second/pallas_call | solution.py:333
Async XLA Ops:
  0.0 46.0 %copy-start = (f32[384,384]{1,0:T(8,128)S(1)}, f32[384,384]{1,0:T(8,128)}, u32[]{:S(2)}) copy-start(f32[384,384]{1,0:T(8,128)} %grad_factor.3) | copy-start | bytes 1769476
  0.0 1.0 copy-start.1
  30.6 15.5 %copy-start.2 = (f32[128,384]{1,0:T(8,128)S(1)}, f32[128,384]{1,0:T(8,128)}, u32[]{:S(2)}) copy-start(f32[128,384]{1,0:T(8,128)} %g.3) | copy-start | bytes 589828
